TPU v7x, 32 devices: a whole 2x2x4 slice. The times are simulated.
32 devices in a mesh: seq: 8 (over z, y), tensor: 4 (over x, core).
Axes of the slice: x: 2, y: 2, z: 4, core: 2. Of those that a mesh axis runs over, the one named last changes fastest.
Arguments:
- fixed_point: bfloat16 [1024, 4096], P(('seq', 'tensor')), may hold values from -6 to 6
- incoming: bfloat16 [1024, 4096], P(('seq', 'tensor')), may hold values from -6 to 6
- norm_gain: float32 [4096], replicated, may hold values from 0.1 to 1.9
- query_weight: bfloat16 [4096, 4096], P(None, 'tensor'), may hold values from -0.21875 to 0.21875, as said below
- key_weight: bfloat16 [4096, 4096], P(None, 'tensor'), may hold values from -0.265625 to 0.265625, as said below
- value_weight: bfloat16 [4096, 4096], P(None, 'tensor'), may hold values from -0.09375 to 0.09375
- out_weight: bfloat16 [4096, 4096], P('tensor'), may hold values from -0.09375 to 0.09375
- layout: int32 [16, 16], replicated, may hold values 0 or 1
Outputs:
- adjoint: float32 [1024, 4096], P(('seq', 'tensor'))
- gain_grad: float32 [4096], replicated
Inputs may be any that keep to these rules, and one draw needn't show every extreme that they name: `query_weight`: entries of the columns of each head are independent; their spread may differ between heads. `key_weight`: entries are independent within a draw; columns of some heads may follow the same head's columns of query_weight. `layout`: A key block strictly before a query block is attended where the entry at row query block, column key block is 1; a block always attends itself causally; entries on or above the diagonal are not read.
All inputs are finite; a program needn't handle non-finite values.
Results may differ from a plain program's by a relative error of at most 0.03.
Values may be sent and summed in bfloat16 or wider, within the bound.
A program may use at most 128 MiB of HBM per device.

v0:
```python
import jax
import jax.numpy as jnp
from jax import lax
from jax.sharding import PartitionSpec as P

HEAD_DIM = 128
BLK = 64
ITERS = 2
EPS = 1e-05
THETA = 10000.0
MASKED = -1e30


def rope_tables(positions):
    freq = THETA ** (-jnp.arange(0, HEAD_DIM, 2, dtype=jnp.float32) / HEAD_DIM)
    angle = positions.astype(jnp.float32)[:, None] * freq[None, :]
    cosine = jnp.concatenate([jnp.cos(angle), jnp.cos(angle)], axis=1)[:, None, :]
    sine = jnp.concatenate([jnp.sin(angle), jnp.sin(angle)], axis=1)[:, None, :]
    return (cosine, sine)


def rotate(values, cosine, sine):
    half = HEAD_DIM // 2
    turned = jnp.concatenate([-values[..., half:], values[..., :half]], axis=-1)
    return values * cosine + turned * sine


def rotate_back(values, cosine, sine):
    half = HEAD_DIM // 2
    weighted = values * sine
    turned = jnp.concatenate([weighted[..., half:], -weighted[..., :half]], axis=-1)
    return values * cosine + turned


def expand_blocks(chosen):
    return jnp.repeat(jnp.repeat(chosen, BLK, axis=0), BLK, axis=1)


def pair_mask(query_pos, key_pos, chosen):
    query_block = (query_pos // BLK)[:, None]
    key_block = (key_pos // BLK)[None, :]
    earlier = (key_block < query_block) & chosen
    same = (key_block == query_block) & (key_pos[None, :] <= query_pos[:, None])
    return earlier | same


def body(
    fixed_point, incoming, norm_gain, query_weight, key_weight, value_weight, out_weight, layout
):
    local_rows, model_width = fixed_point.shape
    head_width = query_weight.shape[1]
    head_count = head_width // HEAD_DIM
    seq_tokens = local_rows * lax.axis_size("tensor")
    seq_length = seq_tokens * lax.axis_size("seq")
    seq_index = lax.axis_index("seq")
    score_scale = HEAD_DIM ** (-0.5)
    contract_last = (((1,), (1,)), ((), ()))
    head_shape = (seq_tokens, head_count, HEAD_DIM)
    point = fixed_point.astype(jnp.float32)
    inv_rms = lax.rsqrt(jnp.mean(point * point, axis=1, keepdims=True) + EPS)
    scaled = point * inv_rms
    normed = (norm_gain * scaled).astype(jnp.bfloat16)
    project_piece = lax.all_gather(normed, "tensor", axis=0, tiled=True)
    projected = jnp.concatenate(
        [
            jnp.dot(project_piece, query_weight, preferred_element_type=jnp.float32),
            jnp.dot(project_piece, key_weight, preferred_element_type=jnp.float32),
            jnp.dot(project_piece, value_weight, preferred_element_type=jnp.float32),
        ],
        axis=1,
    )
    positions = seq_index * seq_tokens + jnp.arange(seq_tokens, dtype=jnp.int32)
    cosine, sine = rope_tables(positions)
    queries = rotate(projected[:, :head_width].reshape(head_shape), cosine, sine).astype(
        jnp.bfloat16
    )
    keys = rotate(
        projected[:, head_width : 2 * head_width].reshape(head_shape), cosine, sine
    ).astype(jnp.bfloat16)
    values = projected[:, 2 * head_width :].reshape(head_shape).astype(jnp.bfloat16)
    block_rows = seq_tokens // BLK
    block_count = seq_length // BLK
    first_block = seq_index * block_rows
    key_positions = jnp.arange(seq_length, dtype=jnp.int32)
    chosen_rows = (
        lax.dynamic_slice(layout, (first_block, jnp.int32(0)), (block_rows, block_count)) > 0
    )
    allowed = pair_mask(positions, key_positions, expand_blocks(chosen_rows))
    keys_all, values_all = (
        lax.all_gather(keys, "seq", axis=0, tiled=True),
        lax.all_gather(values, "seq", axis=0, tiled=True),
    )
    scores = (
        jnp.einsum("qhd,khd->hqk", queries, keys_all, preferred_element_type=jnp.float32)
        * score_scale
    )
    scores = jnp.where(allowed[None], scores, MASKED)
    log_norm = jax.nn.logsumexp(scores, axis=2, keepdims=True)
    probs = jnp.exp(scores - log_norm)
    probs_low = probs.astype(jnp.bfloat16)
    attended = jnp.einsum(
        "hqk,khd->qhd", probs_low, values_all, preferred_element_type=jnp.float32
    ).astype(jnp.bfloat16)
    cotangent = incoming.astype(jnp.float32)
    adjoint = cotangent
    gain_grad = jnp.zeros((model_width,), jnp.float32)
    for term_index in range(ITERS):
        grad_out = lax.dot_general(
            lax.all_gather(cotangent.astype(jnp.bfloat16), "tensor", axis=0, tiled=True),
            out_weight,
            contract_last,
            preferred_element_type=jnp.float32,
        )
        grad_low = grad_out.astype(jnp.bfloat16).reshape(head_shape)
        delta = jnp.sum(grad_low.astype(jnp.float32) * attended.astype(jnp.float32), axis=2)
        grad_probs = jnp.einsum(
            "qhd,khd->hqk", grad_low, values_all, preferred_element_type=jnp.float32
        )
        grad_scores = (probs * (grad_probs - delta.T[:, :, None])).astype(jnp.bfloat16)
        grad_query = (
            jnp.einsum("hqk,khd->qhd", grad_scores, keys_all, preferred_element_type=jnp.float32)
            * score_scale
        )
        key_part = (
            jnp.einsum("hqk,qhd->khd", grad_scores, queries, preferred_element_type=jnp.float32)
            * score_scale
        )
        value_part = jnp.einsum(
            "hqk,qhd->khd", probs_low, grad_low, preferred_element_type=jnp.float32
        )
        key_grads = lax.psum_scatter(
            jnp.concatenate(
                [
                    key_part.reshape(seq_tokens * lax.axis_size("seq"), head_width),
                    value_part.reshape(seq_tokens * lax.axis_size("seq"), head_width),
                ],
                axis=1,
            ).astype(jnp.bfloat16),
            "seq",
            scatter_dimension=0,
            tiled=True,
        ).astype(jnp.float32)
        grad_key = key_grads[:, :head_width].reshape(head_shape)
        grad_value = key_grads[:, head_width:].reshape(head_shape)
        query_low = (
            rotate_back(grad_query, cosine, sine)
            .astype(jnp.bfloat16)
            .reshape(seq_tokens, head_width)
        )
        key_low = (
            rotate_back(grad_key, cosine, sine).astype(jnp.bfloat16).reshape(seq_tokens, head_width)
        )
        value_low = grad_value.astype(jnp.bfloat16).reshape(seq_tokens, head_width)
        total = lax.dot_general(
            query_low, query_weight, contract_last, preferred_element_type=jnp.float32
        )
        total = total + lax.dot_general(
            key_low, key_weight, contract_last, preferred_element_type=jnp.float32
        )
        total = total + lax.dot_general(
            value_low, value_weight, contract_last, preferred_element_type=jnp.float32
        )
        grad_normed = lax.psum_scatter(
            total.astype(jnp.bfloat16), "tensor", scatter_dimension=0, tiled=True
        ).astype(jnp.float32)
        gain_term = jnp.sum(grad_normed * scaled, axis=0)
        gain_grad = gain_grad + lax.psum(gain_term, ("seq", "tensor"))
        weighted = norm_gain * grad_normed
        inner = jnp.sum(weighted * scaled, axis=1, keepdims=True)
        cotangent = inv_rms * (weighted - scaled * (inner / model_width))
        adjoint = adjoint + cotangent
    return (adjoint, gain_grad * seq_length ** (-0.5))


def solution(mesh):
    in_specs = (
        P(("seq", "tensor"), None),
        P(("seq", "tensor"), None),
        P(),
        P(None, "tensor"),
        P(None, "tensor"),
        P(None, "tensor"),
        P("tensor", None),
        P(),
    )
    out_specs = (P(("seq", "tensor"), None), P())
    return jax.shard_map(body, mesh=mesh, in_specs=in_specs, out_specs=out_specs, check_vma=False)
```

profile of v0, /device:TPU:0, one launch (start us, length us, event | category | flops | bytes accessed | tf_op | source)
XLA Modules:
  0.0 525.8 jit_solution(4524562414362292619)
XLA Ops:
  7.2 1.1 fusion.20
  8.9 1.8 fusion.17
  12.0 18.3 %all-gather.6.cloned.1.call-done = bf16[128,4096]{1,0:T(8,128)(2,1)} async-done(((bf16[32,4096]{1,0:T(8,128)(2,1)}), bf16[128,4096]{1,0:T(8,128)(2,1)}) %all-gather.6.cloned.1.call-update) | async-done | bytes 1048592 | tf_op jit(solution)/shard_map/all_gather | solution.py:63
  30.3 5.0 convolution_bitcast_fusion.3
  35.4 4.8 convolution_bitcast_fusion.2
  40.6 1.1 fusion.30
  41.7 4.7 fusion.6
  49.0 6.6 %convolution_convert_fusion.5 = bf16[128,1024]{1,0:T(8,128)(2,1)S(1)} fusion(bf16[128,4096]{1,0:T(8,128)(2,1)} %all-gather.10.cloned.1.call-done, bf16[1024,4096]{1,0:T(8,128)(2,1)} %param.14), kind=kOutput, calls=%fused_computation.28 | convolution fusion | flops 1073872896 | bytes 9699328 | tf_op jit(solution)/shard_map/dot_general | solution.py:108
  55.8 44.6 %all-gather.8.cloned.1.call-done = bf16[1024,8,128]{2,0,1:T(8,128)(2,1)} async-done(((bf16[128,8,128]{2,0,1:T(8,128)(2,1)}), bf16[1024,8,128]{2,0,1:T(8,128)(2,1)}) %all-gather.8.cloned.1.call-update) | async-done | bytes 2097168 | tf_op jit(solution)/shard_map/all_gather | solution.py:90
  100.5 2.5 fusion.2
  103.0 1.1 exponential_reduce_fusion
  105.0 2.1 convolution_convert_fusion.1
  107.1 43.1 %all-gather.12.cloned.1.call-done = bf16[1024,8,128]{2,0,1:T(8,128)(2,1)} async-done(((bf16[128,8,128]{2,0,1:T(8,128)(2,1)}), bf16[1024,8,128]{2,0,1:T(8,128)(2,1)}) %all-gather.12.cloned.1.call-update) | async-done | bytes 2097168 | tf_op jit(solution)/shard_map/all_gather | solution.py:91
  150.2 3.4 multiply_reduce_fusion.1
  153.6 3.3 multiply_convert_fusion.3
  156.9 1.3 copy-done.6
  159.8 2.4 pad_maximum_fusion
  162.3 6.6 %copy.113 = bf16[1024,2048]{1,0:T(8,128)(2,1)} copy(bf16[1024,2048]{0,1:T(8,128)(2,1)} %pad_maximum_fusion) | data formatting | bytes 8388608
  170.4 3.1 broadcast_multiply_fusion.1
  173.6 8.1 %fusion.46 = f32[128,4096]{1,0:T(8,128)} fusion(bf16[128,1024]{0,1:T(8,128)(2,1)S(1)} %bitcast.126, bf16[4096,1024]{1,0:T(8,128)(2,1)} %param.11), kind=kOutput, calls=%fused_computation.123 | convolution fusion | flops 1073741824 | bytes 10747904 | tf_op jit(solution)/shard_map/dot_general | solution.py:154
  181.7 74.1 %reduce-scatter.13.cloned.1.call-done = bf16[128,2048]{1,0:T(8,128)(2,1)} async-done(((bf16[1024,2048]{1,0:T(8,128)(2,1)}), bf16[128,2048]{1,0:T(8,128)(2,1)}) %reduce-scatter.13.cloned.1.call-update) | async-done | bytes 524304
  258.4 1.0 copy.100
  259.4 1.1 fusion.24
  260.5 6.9 %convolution_add_fusion.3 = f32[128,4096]{1,0:T(8,128)S(1)} fusion(f32[128,4096]{1,0:T(8,128)} %fusion.46, bf16[128,1024]{0,1:T(8,128)(2,1)S(1)} %fusion.24, bf16[4096,1024]{1,0:T(8,128)(2,1)} %param.12), kind=kOutput, calls=%fused_computation.3 | convolution fusion | flops 1074266112 | bytes 12845056 | tf_op jit(solution)/shard_map/dot_general | solution.py:157
  267.5 7.3 %fusion = bf16[128,4096]{1,0:T(8,128)(2,1)} fusion(f32[128,4096]{1,0:T(8,128)S(1)} %convolution_add_fusion.3, bf16[4096,1024]{1,0:T(8,128)(2,1)} %param.13, bf16[128,2048]{1,0:T(8,128)(2,1)S(1)} %copy-done.19), kind=kOutput, calls=%fused_computation.4 | convolution fusion | flops 1074790400 | bytes 11796480 | tf_op jit(solution)/shard_map/dot_general | solution.py:160
  274.9 24.6 %reduce-scatter.9.cloned.1.call-done = bf16[32,4096]{1,0:T(8,128)(2,1)} async-done(((bf16[128,4096]{1,0:T(8,128)(2,1)}), bf16[32,4096]{1,0:T(8,128)(2,1)}) %reduce-scatter.9.cloned.1.call-update) | async-done | bytes 262160 | tf_op jit(solution)/shard_map/reduce_scatter | solution.py:163
  299.5 1.8 fusion.21
  301.2 1.8 fusion.35
  303.3 16.6 %all-gather.14.cloned.1.call-done = bf16[128,4096]{1,0:T(8,128)(2,1)} async-done(((bf16[32,4096]{1,0:T(8,128)(2,1)}), bf16[128,4096]{1,0:T(8,128)(2,1)}) %all-gather.14.cloned.1.call-update) | async-done | bytes 1048592 | tf_op jit(solution)/shard_map/all_gather | solution.py:109
  319.9 7.3 %convolution_convert_fusion.3 = bf16[128,1024]{1,0:T(8,128)(2,1)} fusion(bf16[128,4096]{1,0:T(8,128)(2,1)} %all-gather.14.cloned.1.call-done, bf16[1024,4096]{1,0:T(8,128)(2,1)} %param.14), kind=kOutput, calls=%fused_computation.26 | convolution fusion | flops 1073872896 | bytes 9699328 | tf_op jit(solution)/shard_map/dot_general | solution.py:108
  327.3 1.1 copy.101
  329.2 1.4 copy-done.2
  330.6 3.3 multiply_convert_fusion.1
  333.9 1.4 copy-done.7
  336.0 2.5 pad_maximum_fusion.1
  338.5 6.5 %copy.115 = bf16[1024,2048]{1,0:T(8,128)(2,1)} copy(bf16[1024,2048]{0,1:T(8,128)(2,1)} %pad_maximum_fusion.1) | data formatting | bytes 8388608
  345.3 1.3 copy-done.4
  346.6 2.4 broadcast_multiply_fusion
  349.2 6.5 %fusion.47 = f32[128,4096]{1,0:T(8,128)S(1)} fusion(bf16[128,1024]{0,1:T(8,128)(2,1)S(1)} %bitcast.125, bf16[4096,1024]{1,0:T(8,128)(2,1)} %param.11), kind=kOutput, calls=%fused_computation.124 | convolution fusion | flops 1073741824 | bytes 10747904 | tf_op jit(solution)/shard_map/dot_general | solution.py:154
  355.7 77.8 %reduce-scatter.15.cloned.1.call-done = bf16[128,2048]{1,0:T(8,128)(2,1)} async-done(((bf16[1024,2048]{1,0:T(8,128)(2,1)}), bf16[128,2048]{1,0:T(8,128)(2,1)}) %reduce-scatter.15.cloned.1.call-update) | async-done | bytes 524304
  435.3 1.0 copy.106
  436.3 1.1 fusion.26
  437.4 6.3 %convolution_add_fusion.1 = f32[128,4096]{1,0:T(8,128)S(1)} fusion(f32[128,4096]{1,0:T(8,128)S(1)} %fusion.47, bf16[128,1024]{0,1:T(8,128)(2,1)S(1)} %fusion.26, bf16[4096,1024]{1,0:T(8,128)(2,1)} %param.12), kind=kOutput, calls=%fused_computation.1 | convolution fusion | flops 1074266112 | bytes 12845056 | tf_op jit(solution)/shard_map/dot_general | solution.py:157
  443.8 7.3 %fusion.1 = bf16[128,4096]{1,0:T(8,128)(2,1)} fusion(f32[128,4096]{1,0:T(8,128)S(1)} %convolution_add_fusion.1, bf16[4096,1024]{1,0:T(8,128)(2,1)} %param.13, bf16[128,2048]{1,0:T(8,128)(2,1)S(1)} %copy-done.20), kind=kOutput, calls=%fused_computation.5 | convolution fusion | flops 1074790400 | bytes 11796480 | tf_op jit(solution)/shard_map/dot_general | solution.py:160
  451.1 24.6 %reduce-scatter.11.cloned.1.call-done = bf16[32,4096]{1,0:T(8,128)(2,1)} async-done(((bf16[128,4096]{1,0:T(8,128)(2,1)}), bf16[32,4096]{1,0:T(8,128)(2,1)}) %reduce-scatter.11.cloned.1.call-update) | async-done | bytes 262160 | tf_op jit(solution)/shard_map/reduce_scatter | solution.py:163
  475.7 1.3 fusion.22
  477.0 39.4 %psum.16 = f32[4096]{0:T(1024)S(1)} all-reduce(f32[4096]{0:T(1024)S(1)} %add.119), channel_id=1, replica_groups=mesh['seq'=8,'tensor'=4] {'seq','tensor'}, use_global_device_ids=true, to_apply=%region_12.13 | all-reduce | flops 4096 | bytes 32768 | tf_op jit(solution)/shard_map/psum | solution.py:167
  517.0 2.0 fusion.15
  (123 shorter events, 16.4 us)
Async XLA Ops:
  7.2 23.1 %all-gather.6.cloned.1.call-start = ((), (), s32[]{:S(2)}) async-start(), calls=%async_computation.4 | async-start | bytes 1310720 | tf_op jit(solution)/shard_map/all_gather | solution.py:63
  8.3 0.6 copy-start.25
  10.7 38.3 %all-gather.10.cloned.1.call-start = ((), (), s32[]{:S(2)}) async-start(), calls=%async_computation.6 | async-start | bytes 1310720 | tf_op jit(solution)/shard_map/all_gather | solution.py:109
  11.5 89.0 %all-gather.8.cloned.1.call-start = ((), (), s32[]{:S(2)}) async-start(), calls=%async_computation.5 | async-start | bytes 2359296 | tf_op jit(solution)/shard_map/all_gather | solution.py:90
  12.0 28.6 %copy-start.12 = (f32[128,128]{1,0:T(8,128)}, f32[128,128]{1,0:T(8,128)S(1)}, u32[]{:S(2)}) copy-start(f32[128,128]{1,0:T(8,128)S(1)} %get-tuple-element.23) | copy-start | bytes 196612
  30.3 5.1 copy-start.3
  41.7 108.5 %all-gather.12.cloned.1.call-start = ((), (), s32[]{:S(2)}) async-start(), calls=%async_computation.7 | async-start | bytes 2359296 | tf_op jit(solution)/shard_map/all_gather | solution.py:91
  47.2 208.6 %reduce-scatter.13.cloned.1.call-start = ((), (), s32[]{:S(2)}) async-start(), calls=%async_computation.11 | async-start | bytes 4718592
  103.0 2.0 copy-start
  104.1 49.4 %copy-start.23 = (f32[8,128]{1,0:T(8,128)}, f32[8,128]{1,0:T(8,128)S(1)}, u32[]{:S(2)}) copy-start(f32[8,128]{1,0:T(8,128)S(1)} %log_add_fusion) | copy-start | bytes 12292
  150.2 3.4 copy-start.1
  156.9 1.4 copy-start.6
  158.2 1.6 copy-start.8
  168.9 130.6 %reduce-scatter.9.cloned.1.call-start = ((), (), s32[]{:S(2)}) async-start(), calls=%async_computation.8 | async-start | bytes 1310720 | tf_op jit(solution)/shard_map/reduce_scatter | solution.py:163
  170.3 3.2 copy-start.17
  170.4 11.3 %copy-start.15 = (f32[128,128]{0,1:T(8,128)}, f32[128,128]{0,1:T(8,128)S(1)}, u32[]{:S(2)}) copy-start(f32[128,128]{0,1:T(8,128)S(1)} %copy.94) | copy-start | bytes 196612
  260.5 6.9 %copy-start.19 = (bf16[128,2048]{1,0:T(8,128)(2,1)S(1)}, bf16[128,2048]{1,0:T(8,128)(2,1)}, u32[]{:S(2)}) copy-start(bf16[128,2048]{1,0:T(8,128)(2,1)} %reduce-scatter.13.cloned.1.call-done) | copy-start | bytes 1572868
  267.5 32.0 %copy-start.5 = (bf16[32,4096]{1,0:T(8,128)(2,1)S(1)}, bf16[32,4096]{1,0:T(8,128)(2,1)}, u32[]{:S(2)}) copy-start(bf16[32,4096]{1,0:T(8,128)(2,1)} %param.8) | copy-start | bytes 786436
  267.5 32.0 %copy-start.21 = (f32[4096]{0:T(1024)S(1)}, f32[4096]{0:T(1024)}, u32[]{:S(2)}) copy-start(f32[4096]{0:T(1024)} %param.10) | copy-start | bytes 49156
  267.5 32.0 %copy-start.26 = (f32[32]{0:T(128)S(1)}, f32[32]{0:T(128)}, u32[]{:S(2)}) copy-start(f32[32]{0:T(128)} %copy-done.25) | copy-start | bytes 388
  274.9 45.1 %all-gather.14.cloned.1.call-start = ((), (), s32[]{:S(2)}) async-start(), calls=%async_computation.9 | async-start | bytes 1310720 | tf_op jit(solution)/shard_map/all_gather | solution.py:109
  301.2 18.7 %copy-start.28 = (f32[32]{0:T(128)}, f32[32]{0:T(128)S(1)}, u32[]{:S(2)}) copy-start(f32[32]{0:T(128)S(1)} %broadcast_multiply_fusion.8) | copy-start | bytes 388
  303.1 25.3 %copy-start.10 = (f32[128,8,128]{0,2,1:T(8,128)S(1)}, f32[128,8,128]{0,2,1:T(8,128)}, u32[]{:S(2)}) copy-start(f32[128,8,128]{0,2,1:T(8,128)} %get-tuple-element.29) | copy-start | bytes 1572868
  303.1 130.4 %reduce-scatter.15.cloned.1.call-start = ((), (), s32[]{:S(2)}) async-start(), calls=%async_computation.12 | async-start | bytes 4718592
  328.4 2.2 copy-start.2
  328.4 2.2 copy-start.24
  333.9 1.4 copy-start.7
  345.0 1.6 copy-start.4
  345.0 1.6 copy-start.18
  345.1 4.0 copy-start.16
  345.1 130.7 %reduce-scatter.11.cloned.1.call-start = ((), (), s32[]{:S(2)}) async-start(), calls=%async_computation.10 | async-start | bytes 1310720 | tf_op jit(solution)/shard_map/reduce_scatter | solution.py:163
  349.2 85.6 %copy-start.13 = (f32[128,128]{1,0:T(8,128)S(1)}, f32[128,128]{1,0:T(8,128)}, u32[]{:S(2)}) copy-start(f32[128,128]{1,0:T(8,128)} %copy-done.12) | copy-start | bytes 196612
  355.7 80.6 %copy-start.14 = (f32[128,128]{0,1:T(8,128)S(1)}, f32[128,128]{0,1:T(8,128)}, u32[]{:S(2)}) copy-start(f32[128,128]{0,1:T(8,128)} %copy.122) | copy-start | bytes 196612
  437.4 6.4 %copy-start.20 = (bf16[128,2048]{1,0:T(8,128)(2,1)S(1)}, bf16[128,2048]{1,0:T(8,128)(2,1)}, u32[]{:S(2)}) copy-start(bf16[128,2048]{1,0:T(8,128)(2,1)} %reduce-scatter.15.cloned.1.call-done) | copy-start | bytes 1572868
  443.8 32.0 %copy-start.27 = (f32[32]{0:T(128)S(1)}, f32[32]{0:T(128)}, u32[]{:S(2)}) copy-start(f32[32]{0:T(128)} %copy-done.25) | copy-start | bytes 388
  443.8 33.2 %copy-start.22 = (f32[4096]{0:T(1024)S(1)}, f32[4096]{0:T(1024)}, u32[]{:S(2)}) copy-start(f32[4096]{0:T(1024)} %get-tuple-element.4) | copy-start | bytes 49156
  443.8 73.3 %copy-start.9 = (bf16[32,4096]{1,0:T(8,128)(2,1)S(1)}, bf16[32,4096]{1,0:T(8,128)(2,1)}, u32[]{:S(2)}) copy-start(bf16[32,4096]{1,0:T(8,128)(2,1)} %reduce-scatter.9.cloned.1.call-done) | copy-start | bytes 786436
  443.8 73.2 %copy-start.11 = (bf16[32,4096]{1,0:T(8,128)(2,1)S(1)}, bf16[32,4096]{1,0:T(8,128)(2,1)}, u32[]{:S(2)}) copy-start(bf16[32,4096]{1,0:T(8,128)(2,1)} %param.9) | copy-start | bytes 786436
  443.8 73.2 %copy-start.29 = (f32[32]{0:T(128)S(1)}, f32[32]{0:T(128)}, u32[]{:S(2)}) copy-start(f32[32]{0:T(128)} %copy-done.28) | copy-start | bytes 388
Sparse Core Ops, SparseCore 0:
  10.9 19.4 all-gather.5
  31.9 16.6 all-gather.9
  51.4 49.0 all-gather.7
  102.5 47.5 all-gather.11
  169.0 86.7 reduce-scatter.12
  275.0 24.4 reduce-scatter.8
  303.2 16.6 all-gather.13
  345.2 88.2 reduce-scatter.14
  451.3 24.4 reduce-scatter.10
where the time goes:
time: 531 us; the launch traced here: 526 us
  waiting for transfers between devices  325 us (61%)
  matrix products  93.1 us (18%)
  blocking collectives  39.4 us (7%)
  local copies, waits for them, and re-layouts  28.1 us (5%)
  other arithmetic  24.3 us (5%)
  between operations  14.7 us (3%)
    unnamed x11, waiting for transfers between devices  153 us
    reduce_scatter x2, waiting for transfers between devices, body(): lax.psum_scatter(total.astype(jnp.bfloat16), 'tensor', scatter_dimension=...  49.1 us
    all_gather x1, waiting for transfers between devices, body(): lax.all_gather(keys, 'seq', axis=0, tiled=True)  44.6 us
    all_gather x1, waiting for transfers between devices, body(): lax.all_gather(values, 'seq', axis=0, tiled=True)  43.1 us
    psum x1, blocking collectives, body(): gain_grad = gain_grad + lax.psum(gain_term, ('seq', 'tensor'))  39.4 us
    unnamed x65, local copies, waits for them, and re-layouts  21.1 us
    all_gather x1, waiting for transfers between devices, body(): project_piece = lax.all_gather(normed, 'tensor', axis=0, tiled=True)  18.3 us
    all_gather x2, waiting for transfers between devices, body(): lax.all_gather(cotangent.astype(jnp.bfloat16), 'tensor', axis=0, tiled=True)  16.6 us
  transfers between devices with their start and end apart: 9, of which 8 were waited for; matrix products, arithmetic and copies ran while one was open for 10% of the time, Pallas kernels for 0%

commit v1 on v0

--- a/solution.py
+++ b/solution.py
@@ -164,7 +164,7 @@
             total.astype(jnp.bfloat16), "tensor", scatter_dimension=0, tiled=True
         ).astype(jnp.float32)
         gain_term = jnp.sum(grad_normed * scaled, axis=0)
-        gain_grad = gain_grad + lax.psum(gain_term, ("seq", "tensor"))
+        gain_grad = gain_grad + jnp.sum(lax.all_gather(gain_term, ("seq", "tensor")), axis=0)
         weighted = norm_gain * grad_normed
         inner = jnp.sum(weighted * scaled, axis=1, keepdims=True)
         cotangent = inv_rms * (weighted - scaled * (inner / model_width))

time: 531 us -> 548 us (1.032)
  blocking collectives: 39.4 us -> 79.9 us
  waiting for transfers between devices: 325 us -> 301 us
    all_gather x0 -> x2, blocking collectives: none -> 79.9 us  [body(): lax.all_gather(gain_term, ('seq', 'tensor'))]
    psum x1 -> x0, blocking collectives: 39.4 us -> none  [body(): gain_grad = gain_grad + lax.psum(gain_term, ('seq', 'tensor'))]
    reduce_scatter x2, waiting for transfers between devices: 49.1 us -> 24.6 us  [body(): lax.psum_scatter(total.astype(jnp.bfloat16), 'tensor', scatter_dimension=...]
  transfers between devices with their start and end apart: 9 -> 9, of which waited for: 8 -> 7; matrix products, arithmetic and copies ran while one was open for 10% -> 10% of each run, Pallas kernels for 0% -> 0%
where the time goes in v1:
time: 548 us; the launch traced here: 542 us
  waiting for transfers between devices  301 us (55%)
  matrix products  93.1 us (17%)
  blocking collectives  79.9 us (15%)
  local copies, waits for them, and re-layouts  28.2 us (5%)
  other arithmetic  24.4 us (4%)
  between operations  14.7 us (3%)
    unnamed x11, waiting for transfers between devices  153 us
    all_gather x2, blocking collectives, body(): lax.all_gather(gain_term, ('seq', 'tensor'))  79.9 us
    all_gather x1, waiting for transfers between devices, body(): lax.all_gather(keys, 'seq', axis=0, tiled=True)  44.5 us
    all_gather x1, waiting for transfers between devices, body(): lax.all_gather(values, 'seq', axis=0, tiled=True)  43.1 us
    reduce_scatter x2, waiting for transfers between devices, body(): lax.psum_scatter(total.astype(jnp.bfloat16), 'tensor', scatter_dimension=...  24.6 us
    unnamed x65, local copies, waits for them, and re-layouts  21 us
    all_gather x1, waiting for transfers between devices, body(): project_piece = lax.all_gather(normed, 'tensor', axis=0, tiled=True)  18.3 us
    all_gather x2, waiting for transfers between devices, body(): lax.all_gather(cotangent.astype(jnp.bfloat16), 'tensor', axis=0, tiled=True)  16.8 us
  transfers between devices with their start and end apart: 9, of which 7 were waited for; matrix products, arithmetic and copies ran while one was open for 10% of the time, Pallas kernels for 0%

profile of v1, /device:TPU:0, one launch (start us, length us, event | category | flops | bytes accessed | tf_op | source)
XLA Modules:
  0.0 542.1 jit_solution(15867184542519396919)
XLA Ops:
  7.2 1.1 fusion.20
  8.9 1.8 fusion.17
  11.9 18.3 %all-gather.8.cloned.1.call-done = bf16[128,4096]{1,0:T(8,128)(2,1)} async-done(((bf16[32,4096]{1,0:T(8,128)(2,1)}), bf16[128,4096]{1,0:T(8,128)(2,1)}) %all-gather.8.cloned.1.call-update) | async-done | bytes 1048592 | tf_op jit(solution)/shard_map/all_gather | solution.py:63
  30.2 5.0 convolution_bitcast_fusion.3
  35.3 4.8 convolution_bitcast_fusion.2
  40.5 1.1 fusion.30
  41.7 4.7 fusion.6
  49.1 6.6 %convolution_convert_fusion.5 = bf16[128,1024]{1,0:T(8,128)(2,1)S(1)} fusion(bf16[128,4096]{1,0:T(8,128)(2,1)} %all-gather.12.cloned.1.call-done, bf16[1024,4096]{1,0:T(8,128)(2,1)} %param.14), kind=kOutput, calls=%fused_computation.28 | convolution fusion | flops 1073872896 | bytes 9699328 | tf_op jit(solution)/shard_map/dot_general | solution.py:108
  55.9 44.5 %all-gather.10.cloned.1.call-done = bf16[1024,8,128]{2,0,1:T(8,128)(2,1)} async-done(((bf16[128,8,128]{2,0,1:T(8,128)(2,1)}), bf16[1024,8,128]{2,0,1:T(8,128)(2,1)}) %all-gather.10.cloned.1.call-update) | async-done | bytes 2097168 | tf_op jit(solution)/shard_map/all_gather | solution.py:90
  100.4 2.5 fusion.2
  103.0 1.1 exponential_reduce_fusion
  105.0 2.1 convolution_convert_fusion.1
  107.0 43.1 %all-gather.14.cloned.1.call-done = bf16[1024,8,128]{2,0,1:T(8,128)(2,1)} async-done(((bf16[128,8,128]{2,0,1:T(8,128)(2,1)}), bf16[1024,8,128]{2,0,1:T(8,128)(2,1)}) %all-gather.14.cloned.1.call-update) | async-done | bytes 2097168 | tf_op jit(solution)/shard_map/all_gather | solution.py:91
  150.1 3.4 multiply_reduce_fusion.1
  153.5 3.3 multiply_convert_fusion.3
  156.9 1.3 copy-done.6
  159.8 2.4 pad_maximum_fusion
  162.2 6.6 %copy.139 = bf16[1024,2048]{1,0:T(8,128)(2,1)} copy(bf16[1024,2048]{0,1:T(8,128)(2,1)} %pad_maximum_fusion) | data formatting | bytes 8388608
  169.9 3.1 broadcast_multiply_fusion.1
  173.1 8.1 %fusion.46 = f32[128,4096]{1,0:T(8,128)} fusion(bf16[128,1024]{0,1:T(8,128)(2,1)S(1)} %bitcast.126, bf16[4096,1024]{1,0:T(8,128)(2,1)} %param.11), kind=kOutput, calls=%fused_computation.123 | convolution fusion | flops 1073741824 | bytes 10747904 | tf_op jit(solution)/shard_map/dot_general | solution.py:154
  181.2 74.6 %reduce-scatter.13.cloned.1.call-done = bf16[128,2048]{1,0:T(8,128)(2,1)} async-done(((bf16[1024,2048]{1,0:T(8,128)(2,1)}), bf16[128,2048]{1,0:T(8,128)(2,1)}) %reduce-scatter.13.cloned.1.call-update) | async-done | bytes 524304
  258.4 1.0 copy.126
  259.4 1.1 fusion.24
  260.6 6.9 %convolution_add_fusion.3 = f32[128,4096]{1,0:T(8,128)S(1)} fusion(f32[128,4096]{1,0:T(8,128)} %fusion.46, bf16[128,1024]{0,1:T(8,128)(2,1)S(1)} %fusion.24, bf16[4096,1024]{1,0:T(8,128)(2,1)} %param.12), kind=kOutput, calls=%fused_computation.3 | convolution fusion | flops 1074266112 | bytes 12845056 | tf_op jit(solution)/shard_map/dot_general | solution.py:157
  267.5 7.3 %fusion = bf16[128,4096]{1,0:T(8,128)(2,1)} fusion(f32[128,4096]{1,0:T(8,128)S(1)} %convolution_add_fusion.3, bf16[4096,1024]{1,0:T(8,128)(2,1)} %param.13, bf16[128,2048]{1,0:T(8,128)(2,1)S(1)} %copy-done.19), kind=kOutput, calls=%fused_computation.4 | convolution fusion | flops 1074790400 | bytes 11796480 | tf_op jit(solution)/shard_map/dot_general | solution.py:160
  274.9 24.6 %reduce-scatter.9.cloned.1.call-done = bf16[32,4096]{1,0:T(8,128)(2,1)} async-done(((bf16[128,4096]{1,0:T(8,128)(2,1)}), bf16[32,4096]{1,0:T(8,128)(2,1)}) %reduce-scatter.9.cloned.1.call-update) | async-done | bytes 262160 | tf_op jit(solution)/shard_map/reduce_scatter | solution.py:163
  299.5 1.8 fusion.21
  301.3 1.8 fusion.35
  303.2 16.8 %all-gather.16.cloned.1.call-done = bf16[128,4096]{1,0:T(8,128)(2,1)} async-done(((bf16[32,4096]{1,0:T(8,128)(2,1)}), bf16[128,4096]{1,0:T(8,128)(2,1)}) %all-gather.16.cloned.1.call-update) | async-done | bytes 1048592 | tf_op jit(solution)/shard_map/all_gather | solution.py:109
  320.0 7.3 %convolution_convert_fusion.3 = bf16[128,1024]{1,0:T(8,128)(2,1)} fusion(bf16[128,4096]{1,0:T(8,128)(2,1)} %all-gather.16.cloned.1.call-done, bf16[1024,4096]{1,0:T(8,128)(2,1)} %param.14), kind=kOutput, calls=%fused_computation.26 | convolution fusion | flops 1073872896 | bytes 9699328 | tf_op jit(solution)/shard_map/dot_general | solution.py:108
  327.3 1.1 copy.127
  329.2 1.4 copy-done.2
  330.6 3.3 multiply_convert_fusion.1
  334.0 1.4 copy-done.7
  336.1 2.5 pad_maximum_fusion.1
  338.6 6.5 %copy.141 = bf16[1024,2048]{1,0:T(8,128)(2,1)} copy(bf16[1024,2048]{0,1:T(8,128)(2,1)} %pad_maximum_fusion.1) | data formatting | bytes 8388608
  345.4 1.3 copy-done.4
  346.7 2.4 broadcast_multiply_fusion
  349.2 6.5 %fusion.47 = f32[128,4096]{1,0:T(8,128)S(1)} fusion(bf16[128,1024]{0,1:T(8,128)(2,1)S(1)} %bitcast.125, bf16[4096,1024]{1,0:T(8,128)(2,1)} %param.11), kind=kOutput, calls=%fused_computation.124 | convolution fusion | flops 1073741824 | bytes 10747904 | tf_op jit(solution)/shard_map/dot_general | solution.py:154
  355.7 77.8 %reduce-scatter.15.cloned.1.call-done = bf16[128,2048]{1,0:T(8,128)(2,1)} async-done(((bf16[1024,2048]{1,0:T(8,128)(2,1)}), bf16[128,2048]{1,0:T(8,128)(2,1)}) %reduce-scatter.15.cloned.1.call-update) | async-done | bytes 524304
  435.3 1.0 copy.132
  436.3 1.1 fusion.26
  437.5 6.3 %convolution_add_fusion.1 = f32[128,4096]{1,0:T(8,128)S(1)} fusion(f32[128,4096]{1,0:T(8,128)S(1)} %fusion.47, bf16[128,1024]{0,1:T(8,128)(2,1)S(1)} %fusion.26, bf16[4096,1024]{1,0:T(8,128)(2,1)} %param.12), kind=kOutput, calls=%fused_computation.1 | convolution fusion | flops 1074266112 | bytes 12845056 | tf_op jit(solution)/shard_map/dot_general | solution.py:157
  443.9 7.3 %fusion.1 = bf16[128,4096]{1,0:T(8,128)(2,1)} fusion(f32[128,4096]{1,0:T(8,128)S(1)} %convolution_add_fusion.1, bf16[4096,1024]{1,0:T(8,128)(2,1)} %param.13, bf16[128,2048]{1,0:T(8,128)(2,1)S(1)} %copy-done.20), kind=kOutput, calls=%fused_computation.5 | convolution fusion | flops 1074790400 | bytes 11796480 | tf_op jit(solution)/shard_map/dot_general | solution.py:160
  451.2 41.8 %all-gather = f32[131072]{0:T(1024)S(1)} all-gather(f32[4096]{0:T(1024)S(1)} %copy-done.22), channel_id=2, replica_groups=mesh['seq'=8,'tensor'=4] {'seq','tensor'}, dimensions={0}, use_global_device_ids=true | all-gather | bytes 540672 | tf_op jit(solution)/shard_map/all_gather | solution.py:167
  493.2 1.3 fusion.22
  494.5 38.1 %all-gather.1 = f32[131072]{0:T(1024)S(1)} all-gather(f32[4096]{0:T(1024)S(1)} %get-tuple-element.2), channel_id=3, replica_groups=mesh['seq'=8,'tensor'=4] {'seq','tensor'}, dimensions={0}, use_global_device_ids=true | all-gather | bytes 540672 | tf_op jit(solution)/shard_map/all_gather | solution.py:167
  533.3 2.0 fusion.15
  (127 shorter events, 16.2 us)
Async XLA Ops:
  7.2 23.1 %all-gather.8.cloned.1.call-start = ((), (), s32[]{:S(2)}) async-start(), calls=%async_computation.4 | async-start | bytes 1310720 | tf_op jit(solution)/shard_map/all_gather | solution.py:63
  8.3 0.5 copy-start.25
  10.7 38.5 %all-gather.12.cloned.1.call-start = ((), (), s32[]{:S(2)}) async-start(), calls=%async_computation.6 | async-start | bytes 1310720 | tf_op jit(solution)/shard_map/all_gather | solution.py:109
  11.4 89.0 %all-gather.10.cloned.1.call-start = ((), (), s32[]{:S(2)}) async-start(), calls=%async_computation.5 | async-start | bytes 2359296 | tf_op jit(solution)/shard_map/all_gather | solution.py:90
  11.9 28.6 %copy-start.12 = (f32[128,128]{1,0:T(8,128)}, f32[128,128]{1,0:T(8,128)S(1)}, u32[]{:S(2)}) copy-start(f32[128,128]{1,0:T(8,128)S(1)} %get-tuple-element.23) | copy-start | bytes 196612
  30.2 5.1 copy-start.3
  41.6 108.5 %all-gather.14.cloned.1.call-start = ((), (), s32[]{:S(2)}) async-start(), calls=%async_computation.7 | async-start | bytes 2359296 | tf_op jit(solution)/shard_map/all_gather | solution.py:91
  47.1 208.7 %reduce-scatter.13.cloned.1.call-start = ((), (), s32[]{:S(2)}) async-start(), calls=%async_computation.11 | async-start | bytes 4718592
  103.0 2.0 copy-start
  104.1 49.4 %copy-start.23 = (f32[8,128]{1,0:T(8,128)}, f32[8,128]{1,0:T(8,128)S(1)}, u32[]{:S(2)}) copy-start(f32[8,128]{1,0:T(8,128)S(1)} %log_add_fusion) | copy-start | bytes 12292
  150.1 3.4 copy-start.1
  156.9 1.3 copy-start.6
  158.2 1.6 copy-start.8
  168.8 130.7 %reduce-scatter.9.cloned.1.call-start = ((), (), s32[]{:S(2)}) async-start(), calls=%async_computation.8 | async-start | bytes 1310720 | tf_op jit(solution)/shard_map/reduce_scatter | solution.py:163
  169.8 3.2 copy-start.17
  169.9 11.3 %copy-start.15 = (f32[128,128]{0,1:T(8,128)}, f32[128,128]{0,1:T(8,128)S(1)}, u32[]{:S(2)}) copy-start(f32[128,128]{0,1:T(8,128)S(1)} %copy.120) | copy-start | bytes 196612
  260.6 7.0 %copy-start.19 = (bf16[128,2048]{1,0:T(8,128)(2,1)S(1)}, bf16[128,2048]{1,0:T(8,128)(2,1)}, u32[]{:S(2)}) copy-start(bf16[128,2048]{1,0:T(8,128)(2,1)} %reduce-scatter.13.cloned.1.call-done) | copy-start | bytes 1572868
  267.5 32.0 %copy-start.5 = (bf16[32,4096]{1,0:T(8,128)(2,1)S(1)}, bf16[32,4096]{1,0:T(8,128)(2,1)}, u32[]{:S(2)}) copy-start(bf16[32,4096]{1,0:T(8,128)(2,1)} %param.8) | copy-start | bytes 786436
  267.5 32.0 %copy-start.21 = (f32[4096]{0:T(1024)S(1)}, f32[4096]{0:T(1024)}, u32[]{:S(2)}) copy-start(f32[4096]{0:T(1024)} %param.10) | copy-start | bytes 49156
  267.5 32.0 %copy-start.26 = (f32[32]{0:T(128)S(1)}, f32[32]{0:T(128)}, u32[]{:S(2)}) copy-start(f32[32]{0:T(128)} %copy-done.25) | copy-start | bytes 388
  274.9 45.1 %all-gather.16.cloned.1.call-start = ((), (), s32[]{:S(2)}) async-start(), calls=%async_computation.9 | async-start | bytes 1310720 | tf_op jit(solution)/shard_map/all_gather | solution.py:109
  301.3 18.7 %copy-start.28 = (f32[32]{0:T(128)}, f32[32]{0:T(128)S(1)}, u32[]{:S(2)}) copy-start(f32[32]{0:T(128)S(1)} %broadcast_multiply_fusion.7) | copy-start | bytes 388
  303.1 25.3 %copy-start.10 = (f32[128,8,128]{0,2,1:T(8,128)S(1)}, f32[128,8,128]{0,2,1:T(8,128)}, u32[]{:S(2)}) copy-start(f32[128,8,128]{0,2,1:T(8,128)} %get-tuple-element.29) | copy-start | bytes 1572868
  303.1 130.4 %reduce-scatter.15.cloned.1.call-start = ((), (), s32[]{:S(2)}) async-start(), calls=%async_computation.12 | async-start | bytes 4718592
  328.4 2.2 copy-start.2
  328.4 2.2 copy-start.24
  334.0 1.4 copy-start.7
  345.1 1.6 copy-start.4
  345.1 1.6 copy-start.18
  345.1 4.0 copy-start.16
  345.1 148.0 %reduce-scatter.11.cloned.1.call-start = ((), (), s32[]{:S(2)}) async-start(), calls=%async_computation.10 | async-start | bytes 1310720 | tf_op jit(solution)/shard_map/reduce_scatter | solution.py:163
  349.2 85.7 %copy-start.13 = (f32[128,128]{1,0:T(8,128)S(1)}, f32[128,128]{1,0:T(8,128)}, u32[]{:S(2)}) copy-start(f32[128,128]{1,0:T(8,128)} %copy-done.12) | copy-start | bytes 196612
  355.7 80.6 %copy-start.14 = (f32[128,128]{0,1:T(8,128)S(1)}, f32[128,128]{0,1:T(8,128)}, u32[]{:S(2)}) copy-start(f32[128,128]{0,1:T(8,128)} %copy.148) | copy-start | bytes 196612
  437.5 6.4 %copy-start.20 = (bf16[128,2048]{1,0:T(8,128)(2,1)S(1)}, bf16[128,2048]{1,0:T(8,128)(2,1)}, u32[]{:S(2)}) copy-start(bf16[128,2048]{1,0:T(8,128)(2,1)} %reduce-scatter.15.cloned.1.call-done) | copy-start | bytes 1572868
  443.8 7.3 %copy-start.22 = (f32[4096]{0:T(1024)S(1)}, f32[4096]{0:T(1024)}, u32[]{:S(2)}) copy-start(f32[4096]{0:T(1024)} %get-tuple-element.4) | copy-start | bytes 49156
  443.8 49.3 %copy-start.27 = (f32[32]{0:T(128)S(1)}, f32[32]{0:T(128)}, u32[]{:S(2)}) copy-start(f32[32]{0:T(128)} %copy-done.25) | copy-start | bytes 388
  451.1 82.2 %copy-start.9 = (bf16[32,4096]{1,0:T(8,128)(2,1)S(1)}, bf16[32,4096]{1,0:T(8,128)(2,1)}, u32[]{:S(2)}) copy-start(bf16[32,4096]{1,0:T(8,128)(2,1)} %reduce-scatter.9.cloned.1.call-done) | copy-start | bytes 786436
  451.1 82.2 %copy-start.11 = (bf16[32,4096]{1,0:T(8,128)(2,1)S(1)}, bf16[32,4096]{1,0:T(8,128)(2,1)}, u32[]{:S(2)}) copy-start(bf16[32,4096]{1,0:T(8,128)(2,1)} %param.9) | copy-start | bytes 786436
  451.1 82.2 %copy-start.29 = (f32[32]{0:T(128)S(1)}, f32[32]{0:T(128)}, u32[]{:S(2)}) copy-start(f32[32]{0:T(128)} %copy-done.28) | copy-start | bytes 388
Sparse Core Ops, SparseCore 0:
  10.8 19.4 all-gather.7
  31.8 16.6 all-gather.11
  51.3 49.0 all-gather.9
  102.5 47.5 all-gather.13
  168.9 86.8 reduce-scatter.12
  275.0 24.4 reduce-scatter.8
  303.2 16.7 all-gather.15
  345.2 88.2 reduce-scatter.14
  451.3 25.8 reduce-scatter.10
